TPU v7x, 32 devices: a whole 2x2x4 slice. The times are simulated.
32 devices in a mesh: dom: 8 (over z, x), feat: 4 (over y, core).
Axes of the slice: x: 2, y: 2, z: 4, core: 2. Of those that a mesh axis runs over, the one named last changes fastest.
Arguments:
- items: bfloat16 [2048, 1024], P('dom', 'feat'), may hold values from -6 to 6
- self_ids: int32 [2048], P('dom'), may hold values from 0 to 2047
- neighbor_ids: int32 [2048, 50], P('dom'), may hold values from 0 to 2047
- visit_counts: int32 [2048, 50], P('dom'), may hold values from 1 to 63
- w_self: bfloat16 [1024, 1024], P('feat'), may hold values from -0.1875 to 0.1875
- w_neighbor: bfloat16 [1024, 1024], P('feat'), may hold values from -0.75 to 0.75
- bias: float32 [1024], replicated, may hold values from -3 to 3
Outputs:
- embedding: float32 [2048, 1024], P('dom', 'feat')
All inputs are finite; a program needn't handle non-finite values.
Results may differ from a plain program's by a relative error of at most 0.0018.
Values may be sent and summed in bfloat16 or wider, within the bound.
A program may use at most 64 MiB of HBM per device.

v0:
```python
import jax
import jax.numpy as jnp
from jax import lax
from jax.sharding import PartitionSpec as P


def count_block(target_ids, target_weights, width):
    columns = jnp.arange(width, dtype=jnp.int32)
    match = target_ids[:, :, None] == columns[None, None, :]
    block = jnp.sum(jnp.where(match, target_weights[:, :, None], 0.0), axis=1)
    return block.astype(jnp.bfloat16)


def shards(items, self_ids, neighbor_ids, visit_counts, w_self, w_neighbor, bias):
    batch_rows = self_ids.shape[0]
    counts_float = visit_counts.astype(jnp.float32)
    self_column = self_ids[:, None]
    self_weight = jnp.ones((batch_rows, 1), jnp.float32)
    piece = lax.all_gather(items, "dom", axis=0, tiled=True)
    own_block = count_block(self_column, self_weight, piece.shape[0])
    nbr_block = count_block(neighbor_ids, counts_float, piece.shape[0])
    weights = jnp.concatenate([own_block, nbr_block], axis=0)
    sums = jnp.dot(weights, piece, preferred_element_type=jnp.float32)
    own = sums[:batch_rows].astype(jnp.bfloat16)
    nbr_sum = sums[batch_rows:]
    total = jnp.sum(counts_float, axis=1)
    pooled = (nbr_sum / total[:, None]).astype(jnp.bfloat16)
    partial_pre = jnp.dot(own, w_self, preferred_element_type=jnp.float32) + jnp.dot(
        pooled, w_neighbor, preferred_element_type=jnp.float32
    )
    out_share = bias.shape[0] // lax.axis_size("feat")
    column_first = lax.axis_index("feat") * out_share
    pre = lax.psum_scatter(partial_pre, "feat", scatter_dimension=1, tiled=True)
    my_bias = lax.dynamic_slice_in_dim(bias, column_first, out_share, 0)
    hidden = jnp.maximum(pre + my_bias[None, :], 0.0)
    squares = lax.psum(jnp.sum(hidden * hidden, axis=1, keepdims=True), "feat")
    scale = jnp.sqrt(squares / bias.shape[0] + 1e-06)
    return hidden / scale


def solution(mesh):
    placed = (
        P("dom", "feat"),
        P("dom"),
        P("dom", None),
        P("dom", None),
        P("feat", None),
        P("feat", None),
        P(),
    )
    return jax.shard_map(
        shards, mesh=mesh, in_specs=placed, out_specs=P("dom", "feat"), check_vma=False
    )
```

profile of v0, /device:TPU:0, one launch (start us, length us, event | category | flops | bytes accessed | tf_op | source)
XLA Modules:
  0.0 96.0 jit_solution(14140258668490605008)
XLA Ops:
  6.5 0.0 copy-start
  6.5 0.0 copy-start.2
  6.5 0.0 all-gather.2.cloned.1.call-start
  6.5 0.7 all-gather.2.cloned.1.call-update
  7.3 0.0 reduce-scatter.2.cloned.1.call-start
  7.3 0.8 convert_element_type.14
  8.1 0.8 convert_reduce_fusion
  9.0 0.9 select_convert_fusion
  9.9 0.0 copy-done.2
  9.9 17.9 %select_reduce_fusion = bf16[256,2048]{1,0:T(8,128)(2,1)S(1)} fusion(f32[256,50]{0,1:T(8,128)S(1)} %convert_element_type.14, s32[256,50]{0,1:T(8,128)S(1)} %copy-done.2), kind=kLoop, calls=%fused_computation | loop fusion | flops 78118912 | bytes 1150976 | tf_op jit(solution)/shard_map/reduce_sum | solution.py:10
  27.8 24.7 %all-gather.2.cloned.1.call-done = bf16[2048,256]{1,0:T(8,128)(2,1)} async-done(((bf16[256,256]{1,0:T(8,128)(2,1)}), bf16[2048,256]{1,0:T(8,128)(2,1)}) %all-gather.2.cloned.1.call-update) | async-done | bytes 1048592 | tf_op jit(solution)/shard_map/all_gather | solution.py:19
  52.5 1.9 %fusion = f32[512,256]{1,0:T(8,128)S(1)} fusion(bf16[2048,256]{1,0:T(8,128)(2,1)} %all-gather.2.cloned.1.call-done, bf16[256,2048]{1,0:T(8,128)(2,1)S(1)} %select_reduce_fusion, bf16[256,2048]{1,0:T(8,128)(2,1)S(1)} %select_convert_fusion), kind=kOutput, calls=%fused_computation.2 | convolution fusion | flops 541065216 | bytes 3670016 | tf_op jit(solution)/shard_map/dot_general | solution.py:23
  54.4 0.0 copy-done
  54.4 0.0 copy-start.1
  54.5 0.3 fusion.6
  54.8 0.7 copy-done.1
  55.5 1.3 %convolution_add_fusion = f32[256,1024]{1,0:T(8,128)} fusion(f32[256,1024]{1,0:T(8,128)S(1)} %fusion.6, bf16[256,1024]{1,0:T(8,128)(2,1)S(1)} %copy-done.1, f32[512,256]{1,0:T(8,128)S(1)} %fusion, f32[256]{0:T(256)S(1)} %convert_reduce_fusion), kind=kOutput, calls=%fused_computation.8 | convolution fusion | flops 134610944 | bytes 2884608 | tf_op jit(solution)/shard_map/dot_general | solution.py:28
  56.8 0.0 reduce-scatter.2.cloned.1.call-update
  56.9 0.8 dynamic_slice.3
  57.6 22.9 %reduce-scatter.2.cloned.1.call-done = f32[256,256]{1,0:T(8,128)} async-done(((f32[256,1024]{1,0:T(8,128)}), f32[256,256]{1,0:T(8,128)}) %reduce-scatter.2.cloned.1.call-update) | async-done | bytes 262160 | tf_op jit(solution)/shard_map/reduce_scatter | solution.py:33
  80.5 1.1 %multiply_reduce_fusion = f32[256]{0:T(256)S(1)} fusion(f32[256,256]{1,0:T(8,128)} %reduce-scatter.2.cloned.1.call-done, f32[256]{0:T(256)S(1)} %dynamic_slice.3), kind=kLoop, calls=%fused_computation.12 | loop fusion | flops 261888 | bytes 264192 | tf_op jit(solution)/shard_map/reduce_sum | solution.py:36
  81.6 5.8 %psum.7 = f32[256,1]{0,1:T(1,128)S(1)} all-reduce(f32[256,1]{0,1:T(1,128)S(1)} %bitcast.6), channel_id=1, replica_groups=mesh['dom'=8,'feat'=4] {'feat'}, use_global_device_ids=true, to_apply=%region_4.5 | all-reduce | flops 256 | bytes 2048 | tf_op jit(solution)/shard_map/psum | solution.py:36
  87.4 1.8 %fusion.5 = f32[256,256]{1,0:T(8,128)} fusion(f32[256,256]{1,0:T(8,128)} %reduce-scatter.2.cloned.1.call-done, f32[256]{0:T(256)S(1)} %bitcast.5, f32[256]{0:T(256)S(1)} %dynamic_slice.3), kind=kLoop, calls=%fused_computation.14 | loop fusion | flops 196608 | bytes 526336 | tf_op jit(solution)/shard_map/div | solution.py:38
  (1 shorter events, 0.0 us)
Async XLA Ops:
  6.5 47.9 %copy-start = (bf16[256,1024]{1,0:T(8,128)(2,1)S(1)}, bf16[256,1024]{1,0:T(8,128)(2,1)}, u32[]{:S(2)}) copy-start(bf16[256,1024]{1,0:T(8,128)(2,1)} %param.11) | copy-start | bytes 1572868
  6.5 3.4 %copy-start.2 = (s32[256,50]{0,1:T(8,128)S(1)}, s32[256,50]{0,1:T(8,128)}, u32[]{:S(2)}) copy-start(s32[256,50]{0,1:T(8,128)} %param.9) | copy-start | bytes 153604
  6.5 45.9 %all-gather.2.cloned.1.call-start = ((), (), s32[]{:S(2)}) async-start(), calls=%async_computation.1 | async-start | bytes 1179648 | tf_op jit(solution)/shard_map/all_gather | solution.py:19
  7.3 73.3 %reduce-scatter.2.cloned.1.call-start = ((), (), s32[]{:S(2)}) async-start(), calls=%async_computation.2 | async-start | bytes 1310720 | tf_op jit(solution)/shard_map/reduce_scatter | solution.py:33
  54.4 1.0 %copy-start.1 = (bf16[256,1024]{1,0:T(8,128)(2,1)S(1)}, bf16[256,1024]{1,0:T(8,128)(2,1)}, u32[]{:S(2)}) copy-start(bf16[256,1024]{1,0:T(8,128)(2,1)} %param.12) | copy-start | bytes 1572868
Sparse Core Ops, SparseCore 0:
  9.5 42.9 all-gather.1
  57.0 23.4 reduce-scatter.1
where the time goes:
time: 96.4 us; the launch traced here: 96 us
  waiting for transfers between devices  48.3 us (50%)
  other arithmetic  23.3 us (24%)
  between operations  13.5 us (14%)
  blocking collectives  5.76 us (6%)
  matrix products  3.6 us (4%)
  local copies, waits for them, and re-layouts  1.49 us (2%)
    all_gather x1, waiting for transfers between devices, shards(): piece = lax.all_gather(items, 'dom', axis=0, tiled=True)  24.7 us
    reduce_scatter x1, waiting for transfers between devices, shards(): pre = lax.psum_scatter(partial_pre, 'feat', scatter_dimension=1, tiled=True)  22.9 us
    reduce_sum x1, other arithmetic, count_block(): block = jnp.sum(jnp.where(match, target_weights[:, :, None], 0.0), axis=1)  17.9 us
    psum x1, blocking collectives, shards(): squares = lax.psum(jnp.sum(hidden * hidden, axis=1, keepdims=True), 'feat')  5.76 us
    dot_general x1, matrix products, shards(): sums = jnp.dot(weights, piece, preferred_element_type=jnp.float32)  1.95 us
  transfers between devices with their start and end apart: 2, of which 2 were waited for; matrix products, arithmetic and copies ran while one was open for 22% of the time, Pallas kernels for 0%

commit v1 on v0

v1 whole, which is shorter than its diff:
```python
import functools

import jax
import jax.numpy as jnp
from jax import lax
from jax.experimental import pallas as pl
from jax.experimental.pallas import tpu as pltpu
from jax.sharding import PartitionSpec as P

MESH = pl.DeviceIdType.MESH
LANES = 128
GROUP = 8
PARTS = 2


def kernel(
    D, F,
    items_hbm, self_hbm, ids_hbm, cnt_hbm, ws_hbm, wn_hbm, bias_hbm,
    out_ref,
    items, selfs, ids_t, cnt_t, ws, wn, bias,
    ids, cnt, key_s, lo_s, wgt_s, weights, gathered, acc,
    send_a, recv_a, send_b, recv_b, sq_out, sq_in,
    local_sem,
    up_send, up_recv, down_send, down_recv, x_send, x_recv,
    a_send_sem, a_recv_sem, b_send_sem, b_recv_sem, q_send_sem, q_recv_sem,
):
    dom, feat = lax.axis_index("dom"), lax.axis_index("feat")
    Z, H = D // 2, F // 2
    z, x = dom // 2, lax.rem(dom, 2)
    y, c = feat // 2, lax.rem(feat, 2)
    R, FC = items.shape
    nb = selfs.shape[1]
    nbr = ids.shape[1]
    share = out_ref.shape[1]
    slot = key_s.shape[1] // GROUP
    n_hi = D * R // LANES
    part = R // PARTS

    pairs = ((items_hbm, items), (ids_hbm, ids_t), (cnt_hbm, cnt_t), (self_hbm, selfs), (ws_hbm, ws), (wn_hbm, wn), (bias_hbm, bias))
    local = [pltpu.make_async_copy(a, b, local_sem.at[i]) for i, (a, b) in enumerate(pairs)]
    for copy in local:
        copy.start()

    barrier = pltpu.get_barrier_semaphore()

    def greet(d, f):
        pl.semaphore_signal(barrier, inc=1, device_id=(d, f), device_id_type=MESH)

    greet(dom + 1 - 2 * x, feat)

    @pl.when(z > 0)
    def _():
        greet(dom - 2, feat)

    @pl.when(z < Z - 1)
    def _():
        greet(dom + 2, feat)

    for k in range(1, F):
        greet(dom, lax.rem(feat + k, F))

    pl.semaphore_wait(barrier, F + (z > 0).astype(jnp.int32) + (z < Z - 1).astype(jnp.int32))
    local[0].wait()

    def rows_of(block, h):
        return pl.ds(pl.multiple_of(block * R + h * part, part), part)

    def block_copy(block, h, own, send_sem, recv_sem, target):
        dst = gathered.at[rows_of(block, h), :]
        src = items.at[pl.ds(h * part, part), :] if own else dst
        return pltpu.make_async_remote_copy(
            src_ref=src, dst_ref=dst, send_sem=send_sem, recv_sem=recv_sem,
            device_id=(target, feat), device_id_type=MESH,
        )

    def up_copy(s, h):
        i = s * PARTS + h
        return block_copy(dom - 2 * s, h, s == 0, up_send.at[i], up_recv.at[i], dom + 2)

    def down_copy(s, h):
        i = s * PARTS + h
        return block_copy(dom + 2 * s, h, s == 0, down_send.at[i], down_recv.at[i], dom - 2)

    def x_copy(step, h):
        i = (step + Z - 1) * PARTS + h
        return block_copy(dom + 2 * step, h, step == 0, x_send.at[i], x_recv.at[i], dom + 1 - 2 * x)

    def up_arrived(s, h):
        i = s * PARTS + h
        block_copy(dom - 2 * (s + 1), h, False, up_send.at[i], up_recv.at[i], dom).wait_recv()

    def down_arrived(s, h):
        i = s * PARTS + h
        block_copy(dom + 2 * (s + 1), h, False, down_send.at[i], down_recv.at[i], dom).wait_recv()

    def x_arrived(step, h):
        i = (step + Z - 1) * PARTS + h
        block_copy(dom + 1 - 2 * x + 2 * step, h, False, x_send.at[i], x_recv.at[i], dom).wait_recv()

    for h in range(PARTS):
        @pl.when(z < Z - 1)
        def _():
            up_copy(0, h).start()

        @pl.when(z > 0)
        def _():
            down_copy(0, h).start()

        x_copy(0, h).start()

    def forward(s, h):
        @pl.when(z > s)
        def _():
            up_arrived(s, h)

            @pl.when(z < Z - 1)
            def _():
                up_copy(s + 1, h).start()

            x_copy(-(s + 1), h).start()

        @pl.when(z < Z - 1 - s)
        def _():
            down_arrived(s, h)

            @pl.when(z > 0)
            def _():
                down_copy(s + 1, h).start()

            x_copy(s + 1, h).start()

    for copy in local[1:4]:
        copy.wait()
    ids[...] = jnp.transpose(ids_t[...])
    cnt[...] = jnp.transpose(cnt_t[...])
    wgt_s[...] = jnp.zeros_like(wgt_s)
    lo_s[...] = jnp.zeros_like(lo_s)
    key_s[...] = jnp.zeros_like(key_s)
    for j in range(GROUP):
        ids_j = ids[pl.ds(j, nb // GROUP, stride=GROUP), :]
        at = slice(j * slot, j * slot + nbr)
        key_s[:, at] = (ids_j // LANES) * GROUP + j
        lo_s[:, at] = lax.rem(ids_j, LANES)
        wgt_s[:, at] = cnt[pl.ds(j, nb // GROUP, stride=GROUP), :].astype(jnp.float32)

    K = key_s.shape[1]

    def half_group(g):
        key = key_s[pl.ds(g, 1), :]
        low = lo_s[pl.ds(g, 1), :]
        wgt = wgt_s[pl.ds(g, 1), :]
        left = jnp.where(lax.broadcasted_iota(jnp.int32, (n_hi * GROUP, K), 0) == key, wgt, 0.0)
        right = jnp.where(lax.broadcasted_iota(jnp.int32, (LANES, K), 0) == low, 1.0, 0.0)
        return lax.dot_general(
            left.astype(jnp.bfloat16), right.astype(jnp.bfloat16),
            (((1,), (1,)), ((), ())), preferred_element_type=jnp.float32,
        )

    def build(it, carry):
        first, second = half_group(it * 2), half_group(it * 2 + 1)
        at = pl.ds(pl.multiple_of(nb + it * 2 * GROUP, 2 * GROUP), 2 * GROUP)
        for hi in range(n_hi):
            rows = slice(hi * GROUP, (hi + 1) * GROUP)
            tile = jnp.concatenate([first[rows], second[rows]], axis=0)
            weights[at, hi * LANES:(hi + 1) * LANES] = tile.astype(jnp.bfloat16)
        return carry

    groups = nb // (2 * GROUP)
    lax.fori_loop(0, groups // 2, build, 0)
    forward(0, 0)
    lax.fori_loop(groups // 2, groups, build, 0)
    forward(0, 1)
    self_col = jnp.transpose(jnp.broadcast_to(selfs[...], (LANES, nb)))
    lane = lax.broadcasted_iota(jnp.int32, (nb, LANES), 1)
    for hi in range(n_hi):
        hit = jnp.where(self_col == lane + hi * LANES, 1.0, 0.0)
        weights[0:nb, hi * LANES:(hi + 1) * LANES] = hit.astype(jnp.bfloat16)
    total = jnp.sum(cnt[...].astype(jnp.float32), axis=1, keepdims=True)

    def columns(block):
        return weights[:, pl.ds(pl.multiple_of(block * R, R), R)]

    def add(block):
        rows = pl.ds(pl.multiple_of(block * R, R), R)
        acc[...] += jnp.dot(columns(block), gathered[rows, :], preferred_element_type=jnp.float32)

    def add_line(step, z_now, wait):
        @pl.when((z_now + step >= 0) & (z_now + step < Z))
        def _():
            if wait:
                for h in range(PARTS):
                    x_arrived(step, h)
                add(dom + 1 - 2 * x + 2 * step)
            else:
                add(dom + 2 * step)

    acc[...] = jnp.dot(columns(dom), items[...], preferred_element_type=jnp.float32)
    add_line(0, z, True)
    for s in range(Z - 1):
        if s > 0:
            for h in range(PARTS):
                forward(s, h)
        for step in (-(s + 1), s + 1):
            add_line(step, z, False)
        if s > 0:
            for step in (-s, s):
                add_line(step, z, True)
    for step in (-(Z - 1), Z - 1):
        add_line(step, z, True)

    own = acc[0:nb, :].astype(jnp.bfloat16)
    pooled = (acc[nb:2 * nb, :] / total).astype(jnp.bfloat16)
    local[4].wait()
    local[5].wait()
    local[6].wait()

    def project(yy, cc):
        cols = pl.ds(pl.multiple_of((yy * 2 + cc) * share, share), share)
        return jnp.dot(own, ws[:, cols], preferred_element_type=jnp.float32) + jnp.dot(
            pooled, wn[:, cols], preferred_element_type=jnp.float32
        )

    def a_copy(k):
        return pltpu.make_async_remote_copy(
            src_ref=send_a.at[k], dst_ref=recv_a.at[k], send_sem=a_send_sem.at[k], recv_sem=a_recv_sem.at[k],
            device_id=(dom, feat + 1 - 2 * c), device_id_type=MESH,
        )

    def b_copy(k):
        return pltpu.make_async_remote_copy(
            src_ref=send_b.at[k], dst_ref=recv_b.at[k], send_sem=b_send_sem.at[k], recv_sem=b_recv_sem.at[k],
            device_id=(dom, lax.rem(y + k + 1, H) * 2 + c), device_id_type=MESH,
        )

    for k in range(H):
        send_a[k] = project(lax.rem(y + k + 1, H), 1 - c)
        a_copy(k).start()
    mine = None
    for k in range(H):
        here = project(lax.rem(y + k + 1, H), c)
        a_copy(k).wait_recv()
        summed = here + recv_a[k]
        if k < H - 1:
            send_b[k] = summed.astype(jnp.bfloat16)
            b_copy(k).start()
        else:
            mine = summed + bias[:, pl.ds(pl.multiple_of(feat * share, share), share)]
    for k in range(H - 1):
        b_copy(k).wait_recv()
        mine = mine + recv_b[k].astype(jnp.float32)
    hidden = jnp.maximum(mine, 0.0)
    squares = jnp.sum(hidden * hidden, axis=1, keepdims=True)
    row = jnp.transpose(jnp.broadcast_to(squares, (nb, LANES)))[0:GROUP, :]
    sq_out[...] = row

    def q_copy(k):
        return pltpu.make_async_remote_copy(
            src_ref=sq_out, dst_ref=sq_in.at[k - 1], send_sem=q_send_sem.at[k - 1], recv_sem=q_recv_sem.at[k - 1],
            device_id=(dom, lax.rem(feat + k, F)), device_id_type=MESH,
        )

    for k in range(1, F):
        q_copy(k).start()
    for k in range(1, F):
        q_copy(k).wait_recv()
        row = row + sq_in[k - 1]
    scale = lax.rsqrt(row / (share * F) + 1e-06)[0:1, :]
    column = jnp.transpose(jnp.broadcast_to(scale, (LANES, nb)))
    for i in range(share // LANES):
        at = slice(i * LANES, (i + 1) * LANES)
        out_ref[:, at] = hidden[:, at] * column

    for s in range(Z - 1):
        for h in range(PARTS):
            @pl.when((z < Z - 1) & (z >= s))
            def _():
                up_copy(s, h).wait_send()

            @pl.when((z > 0) & (z < Z - s))
            def _():
                down_copy(s, h).wait_send()
    for step in range(-(Z - 1), Z):
        @pl.when((z + step >= 0) & (z + step < Z))
        def _():
            for h in range(PARTS):
                x_copy(step, h).wait_send()
    for k in range(H):
        a_copy(k).wait_send()
    for k in range(H - 1):
        b_copy(k).wait_send()
    for k in range(1, F):
        q_copy(k).wait_send()


def shards(D, F, items, self_ids, neighbor_ids, visit_counts, w_self, w_neighbor, bias):
    R, FC = items.shape
    nb, nbr = neighbor_ids.shape
    out = bias.shape[0]
    share = out // F
    slot = 1 << (nbr - 1).bit_length()
    Z, H = D // 2, F // 2
    lines = (Z - 1) * PARTS
    f32, bf16, i32 = jnp.float32, jnp.bfloat16, jnp.int32
    dma = pltpu.SemaphoreType.DMA
    return pl.pallas_call(
        functools.partial(kernel, D, F),
        out_shape=jax.ShapeDtypeStruct((nb, share), f32),
        in_specs=[pl.BlockSpec(memory_space=pl.ANY)] * 7,
        out_specs=pl.BlockSpec(memory_space=pltpu.VMEM),
        scratch_shapes=[
            pltpu.VMEM((R, FC), bf16),
            pltpu.VMEM((1, nb), i32),
            pltpu.VMEM((nbr, nb), i32),
            pltpu.VMEM((nbr, nb), i32),
            pltpu.VMEM((FC, out), bf16),
            pltpu.VMEM((FC, out), bf16),
            pltpu.VMEM((1, out), f32),
            pltpu.VMEM((nb, nbr), i32),
            pltpu.VMEM((nb, nbr), i32),
            pltpu.VMEM((nb // GROUP, GROUP * slot), i32),
            pltpu.VMEM((nb // GROUP, GROUP * slot), i32),
            pltpu.VMEM((nb // GROUP, GROUP * slot), f32),
            pltpu.VMEM((2 * nb, D * R), bf16),
            pltpu.VMEM((D * R, FC), bf16),
            pltpu.VMEM((2 * nb, FC), f32),
            pltpu.VMEM((H, nb, share), f32),
            pltpu.VMEM((H, nb, share), f32),
            pltpu.VMEM((H - 1, nb, share), bf16),
            pltpu.VMEM((H - 1, nb, share), bf16),
            pltpu.VMEM((GROUP, nb), f32),
            pltpu.VMEM((F - 1, GROUP, nb), f32),
            dma((7,)),
            dma((lines,)), dma((lines,)), dma((lines,)), dma((lines,)),
            dma(((2 * Z - 1) * PARTS,)), dma(((2 * Z - 1) * PARTS,)),
            dma((H,)), dma((H,)), dma((H - 1,)), dma((H - 1,)), dma((F - 1,)), dma((F - 1,)),
        ],
        compiler_params=pltpu.CompilerParams(collective_id=0, has_side_effects=True),
    )(items, self_ids.reshape(1, nb), neighbor_ids.T, visit_counts.T, w_self, w_neighbor, bias.reshape(1, out))


def solution(mesh):
    placed = (
        P("dom", "feat"),
        P("dom"),
        P("dom", None),
        P("dom", None),
        P("feat", None),
        P("feat", None),
        P(),
    )
    return jax.shard_map(
        functools.partial(shards, mesh.shape["dom"], mesh.shape["feat"]),
        mesh=mesh, in_specs=placed, out_specs=P("dom", "feat"), check_vma=False,
    )
```

time: 96.4 us -> 33.2 us (0.34)
  waiting for transfers between devices: 48.3 us -> 0 us
  Pallas kernels: 0 us -> 31.4 us
  other arithmetic: 23.3 us -> 0 us
  between operations: 13.5 us -> 0.01 us
  blocking collectives: 5.76 us -> 0 us
  matrix products: 3.6 us -> 0 us
    pallas_call x0 -> x1, Pallas kernels: none -> 31.4 us  [shards(): pl.pallas_call(functools.partial(kernel, D, F), out_shape=jax.ShapeDtypeS...]
    all_gather x1 -> x0, waiting for transfers between devices: 24.7 us -> none  [shards(): piece = lax.all_gather(items, 'dom', axis=0, tiled=True)]
    reduce_scatter x1 -> x0, waiting for transfers between devices: 22.9 us -> none  [shards(): pre = lax.psum_scatter(partial_pre, 'feat', scatter_dimension=1, tiled=True)]
    reduce_sum x3 -> x0, other arithmetic: 19.8 us -> none  [the longest x1 17.9 us: count_block(): block = jnp.sum(jnp.where(match, target_weights[:, :, None], 0.0), axis=1)]
    psum x1 -> x0, blocking collectives: 5.76 us -> none  [shards(): squares = lax.psum(jnp.sum(hidden * hidden, axis=1, keepdims=True), 'feat')]
    dot_general x3 -> x0, matrix products: 3.6 us -> none  [the longest x1 1.95 us: shards(): sums = jnp.dot(weights, piece, preferred_element_type=jnp.float32)]
    div x1 -> x0, other arithmetic: 1.76 us -> none  [shards(): return hidden / scale]
    convert_element_type x2 -> x0, other arithmetic: 1.74 us -> none  [the longest x1 0.91 us: count_block(): return block.astype(jnp.bfloat16)]
  transfers between devices with their start and end apart: 2 -> 0, of which waited for: 2 -> 0; matrix products, arithmetic and copies ran while one was open for 22% -> 0% of each run, Pallas kernels for 0% -> 0%
where the time goes in v1:
time: 33.2 us; the launch traced here: 33.1 us
  Pallas kernels  31.4 us (95%)
  local copies, waits for them, and re-layouts  1.67 us (5%)
    pallas_call x1, Pallas kernels, shards(): pl.pallas_call(functools.partial(kernel, D, F), out_shape=jax.ShapeDtypeS...  31.4 us
    unnamed x1, local copies, waits for them, and re-layouts  1.67 us

profile of v1, /device:TPU:0, one launch (start us, length us, event | category | flops | bytes accessed | tf_op | source)
XLA Modules:
  0.0 33.1 jit_solution(11099777154404774840)
XLA Ops:
  0.0 31.4 %shard_map.73 = f32[256,256]{1,0:T(8,128)} custom-call(bf16[256,256]{1,0:T(8,128)(2,1)} %items_hbm.1, s32[1,256]{1,0:T(1,128)} %bitcast.7, s32[50,256]{1,0:T(8,128)} %bitcast.4, s32[50,256]{1,0:T(8,128)} %bitcast.5, bf16[256,1024]{1,0:T(8,128)(2,1)} %ws_hbm.1, bf16[256,1024]{1,0:T(8,128)(2,1)} %wn_hbm.1, f32[1,1024]{1,0:T(1,128)} %bitcast.6), custom_call_target="tpu_custom_call" | custom-call | tf_op jit(solution)/shard_map/pallas_call | solution.py:305
  31.4 1.7 %copy.9 = f32[256,256]{1,0:T(8,128)} copy(f32[256,256]{1,0:T(8,128)} %shard_map.73) | data formatting | bytes 524288

commit v2 on v1

--- a/solution.py
+++ b/solution.py
@@ -10,7 +10,7 @@
 MESH = pl.DeviceIdType.MESH
 LANES = 128
 GROUP = 8
-PARTS = 2
+PARTS = 4
 
 
 def kernel(
@@ -165,11 +165,13 @@
             weights[at, hi * LANES:(hi + 1) * LANES] = tile.astype(jnp.bfloat16)
         return carry
 
-    groups = nb // (2 * GROUP)
-    lax.fori_loop(0, groups // 2, build, 0)
-    forward(0, 0)
-    lax.fori_loop(groups // 2, groups, build, 0)
-    forward(0, 1)
+    def build_pair(it, carry):
+        return build(it * 2 + 1, build(it * 2, carry))
+
+    pairs_here = nb // (4 * GROUP)
+    for h in range(PARTS):
+        lax.fori_loop(pairs_here * h // PARTS, pairs_here * (h + 1) // PARTS, build_pair, 0)
+        forward(0, h)
     self_col = jnp.transpose(jnp.broadcast_to(selfs[...], (LANES, nb)))
     lane = lax.broadcasted_iota(jnp.int32, (nb, LANES), 1)
     for hi in range(n_hi):
@@ -304,7 +306,7 @@
     dma = pltpu.SemaphoreType.DMA
     return pl.pallas_call(
         functools.partial(kernel, D, F),
-        out_shape=jax.ShapeDtypeStruct((nb, share), f32),
+        out_shape=pltpu.VMEM((nb, share), f32),
         in_specs=[pl.BlockSpec(memory_space=pl.ANY)] * 7,
         out_specs=pl.BlockSpec(memory_space=pltpu.VMEM),
         scratch_shapes=[

time: 33.2 us -> 30.3 us (0.913)
  Pallas kernels: 31.4 us -> 29.4 us
  local copies, waits for them, and re-layouts: 1.67 us -> 0.71 us
    pallas_call x1, Pallas kernels: 31.4 us -> 29.4 us  [shards(): pl.pallas_call(functools.partial(kernel, D, F), out_shape=pltpu.VMEM((nb,...]
    unnamed x1, local copies, waits for them, and re-layouts: 1.67 us -> 0.71 us
where the time goes in v2:
time: 30.3 us; the launch traced here: 30.2 us
  Pallas kernels  29.4 us (97%)
  local copies, waits for them, and re-layouts  0.71 us (2%)
    pallas_call x1, Pallas kernels, shards(): pl.pallas_call(functools.partial(kernel, D, F), out_shape=pltpu.VMEM((nb,...  29.4 us
    unnamed x1, local copies, waits for them, and re-layouts  0.71 us

profile of v2, /device:TPU:0, one launch (start us, length us, event | category | flops | bytes accessed | tf_op | source)
XLA Modules:
  0.0 30.2 jit_solution(289520428556035324)
XLA Ops:
  0.0 29.4 %shard_map.73 = f32[256,256]{1,0:T(8,128)S(1)} custom-call(bf16[256,256]{1,0:T(8,128)(2,1)} %items_hbm.1, s32[1,256]{1,0:T(1,128)} %bitcast.7, s32[50,256]{1,0:T(8,128)} %bitcast.4, s32[50,256]{1,0:T(8,128)} %bitcast.5, bf16[256,1024]{1,0:T(8,128)(2,1)} %ws_hbm.1, bf16[256,1024]{1,0:T(8,128)(2,1)} %wn_hbm.1, f32[1,1024]{1,0:T(1,128)} %bitcast.6), custom_call_target="tpu_custom_call" | custom-call | tf_op jit(solution)/shard_map/pallas_call | solution.py:307
  29.5 0.7 %copy.9 = f32[256,256]{1,0:T(8,128)} copy(f32[256,256]{1,0:T(8,128)S(1)} %shard_map.73) | data formatting | bytes 524288
